TPU v7x, 32 devices: a whole 2x2x4 slice. The times are simulated.
32 devices in a mesh: sfc: 8 (over z, y), sub: 4 (over x, core).
Axes of the slice: x: 2, y: 2, z: 4, core: 2. Of those that a mesh axis runs over, the one named last changes fastest.
Arguments:
- vectors: float32 [64, 512, 256], P(None, ('sfc', 'sub')), may hold values from -10 to 10
- reaction: float32 [512, 256], P(('sfc', 'sub')), may hold values from 0.5 to 5
Outputs:
- basis: float32 [64, 512, 256], P(None, ('sfc', 'sub'))
- upper: float32 [64, 64], replicated
All inputs are finite; a program needn't handle non-finite values.
Results may differ from a plain program's by a relative error of at most 0.0003.
Values sent between devices are 32-bit elements; how exact they have to be, the bound alone decides.
A program may use at most 64 MiB of HBM per device.

v0:
```python
import math
import jax
import jax.numpy as jnp
from jax import lax
from jax.sharding import PartitionSpec as P

NY = 32
NL = 8
POWERS = 3
DELTA_MASS = 0.5


def with_halo(cells, sides, width):
    for axis, dim in sides:
        count = lax.axis_size(axis)
        ends = count - 1
        head = lax.slice_in_dim(cells, 0, width, axis=dim)
        tail = lax.slice_in_dim(cells, cells.shape[dim] - width, cells.shape[dim], axis=dim)
        cells = jnp.concatenate(
            [
                lax.ppermute(tail, axis, [(i, (i + 1) % count) for i in range(ends)]),
                cells,
                lax.ppermute(head, axis, [((i + 1) % count, i) for i in range(ends)]),
            ],
            axis=dim,
        )
    return cells


def line_tables(count):
    index = jnp.arange(count)
    offset = index[:, None] - index[None, :]
    near = (jnp.abs(offset) == 1).astype(jnp.float32)
    same = (offset == 0).astype(jnp.float32)
    mass = (4.0 * same + near) / 6.0
    stiff = 2.0 * same - near
    return (mass, stiff)


def tables(across, layers):
    mass_across, stiff_across = line_tables(across)
    mass_layers, stiff_layers = line_tables(layers)
    mass_plane = jnp.kron(mass_layers, mass_across)
    stiff_plane = (
        jnp.kron(mass_layers, stiff_across)
        + jnp.kron(stiff_layers, mass_across)
        + DELTA_MASS * mass_plane
    )
    return jnp.concatenate([mass_plane, stiff_plane], axis=1)


def plane_products(field, table):
    plane = table.shape[0]
    both = jnp.einsum("kzp,pq->kzq", field, table, precision=lax.Precision.HIGHEST)
    return (both[..., :plane], both[..., plane:])


def operate(field, reaction, table):
    massed, mixed = plane_products(field, table)
    edge_term = mixed / 6.0 - massed
    padded = with_halo(edge_term, ((("sfc", "sub"), 1),), 1)
    neighbours = padded[:, :-2] + padded[:, 2:]
    return neighbours + 4.0 / 6.0 * mixed + 2.0 * massed + reaction[None] * field


def whole_factor(local):
    gram = jnp.dot(local, local.T, precision=lax.Precision.HIGHEST)
    total = lax.psum(gram, ("sfc", "sub"))
    return jnp.linalg.cholesky(total)


def lower_solve(lower, block):
    return lax.linalg.triangular_solve(lower, block, left_side=True, lower=True)


def per_device(vectors, reaction):
    table = tables(NY, NL)
    field = vectors
    for _ in range(POWERS):
        field = operate(field, reaction, table)
    local = field.reshape(field.shape[0], -1)
    lower_one = whole_factor(local)
    first = lower_solve(lower_one, local)
    lower_two = whole_factor(first)
    second = lower_solve(lower_two, first)
    scale = math.sqrt(lax.axis_size("sfc") * lax.axis_size("sub") * local.shape[1])
    upper = jnp.dot(lower_one, lower_two, precision=lax.Precision.HIGHEST).T / scale
    return ((second * scale).reshape(vectors.shape), upper)


def solution(mesh):
    placed = (P(None, ("sfc", "sub"), None), P(("sfc", "sub"), None))
    return jax.shard_map(
        per_device,
        mesh=mesh,
        in_specs=placed,
        out_specs=(P(None, ("sfc", "sub"), None), P()),
        check_vma=False,
    )
```

profile of v0, /device:TPU:0, one launch (start us, length us, event | category | flops | bytes accessed | tf_op | source)
XLA Modules:
  0.0 152.5 jit_solution(1561632378919360733)
XLA Ops:
  1.6 0.5 copy-done
  2.2 2.3 %convolution_bitcast_fusion = f32[64,16,512]{2,0,1:T(8,128)S(1)} fusion(f32[64,16,256]{2,1,0:T(8,128)S(1)} %copy-done, f32[256,256]{1,0:T(8,128)S(1)} %multiply_add_fusion.1, f32[256,256]{1,0:T(8,128)S(1)} %mul.143), kind=kOutput, calls=%fused_computation.1 | convolution fusion | flops 1610743808 | bytes 3670016 | tf_op jit(solution)/shard_map/kzp,pq->kzq/dot_general | solution.py:54
  4.7 2.4 %collective-permute-start = (f32[64,1,256]{2,0,1:T(8,128)S(1)}, f32[64,1,256]{2,0,1:T(8,128)S(1)}, u32[]{:S(2)}, u32[]{:S(2)}) collective-permute-start(f32[64,1,256]{2,0,1:T(8,128)S(1)} %get-tuple-element.8), channel_id=1, source_target_pairs={{0,1},{1,2},{2,3},{3,4},{4,5},{5,6},{6,7},{7,8},{8,9},{9,10},{10,1... | collective-permute-start | bytes 196616 | tf_op jit(solution)/shard_map/ppermute | solution.py:21
  7.1 1.3 collective-permute-start.1
  8.4 3.9 %collective-permute-done.1 = f32[64,1,256]{2,0,1:T(8,128)S(1)} collective-permute-done((f32[64,1,256]{2,0,1:T(8,128)S(1)}, f32[64,1,256]{2,0,1:T(8,128)S(1)}, u32[]{:S(2)}, u32[]{:S(2)}) %collective-permute-start.1) | collective-permute-done | bytes 65568 | tf_op jit(solution)/shard_map/ppermute | solution.py:23
  12.3 0.8 fusion.11
  13.2 1.8 %fusion.14 = f32[64,16,512]{2,0,1:T(8,128)S(1)} fusion(f32[64,16,256]{2,0,1:T(8,128)S(1)} %fusion.11, f32[256,256]{1,0:T(8,128)S(1)} %multiply_add_fusion.1, f32[256,256]{1,0:T(8,128)S(1)} %mul.143), kind=kOutput, calls=%fused_computation.30 | convolution fusion | flops 1610743808 | bytes 3670016 | tf_op jit(solution)/shard_map/kzp,pq->kzq/dot_general | solution.py:54
  15.2 4.8 %collective-permute-start.2 = (f32[64,1,256]{2,0,1:T(8,128)S(1)}, f32[64,1,256]{2,0,1:T(8,128)S(1)}, u32[]{:S(2)}, u32[]{:S(2)}) collective-permute-start(f32[64,1,256]{2,0,1:T(8,128)S(1)} %get-tuple-element.6), channel_id=1, source_target_pairs={{0,1},{1,2},{2,3},{3,4},{4,5},{5,6},{6,7},{7,8},{8,9},{9,10},{10,1... | collective-permute-start | bytes 196616 | tf_op jit(solution)/shard_map/ppermute | solution.py:21
  20.0 1.3 collective-permute-start.3
  21.4 1.8 %collective-permute-done.3 = f32[64,1,256]{2,0,1:T(8,128)S(1)} collective-permute-done((f32[64,1,256]{2,0,1:T(8,128)S(1)}, f32[64,1,256]{2,0,1:T(8,128)S(1)}, u32[]{:S(2)}, u32[]{:S(2)}) %collective-permute-start.3) | collective-permute-done | bytes 65568 | tf_op jit(solution)/shard_map/ppermute | solution.py:23
  23.2 0.3 fusion.7
  23.5 1.8 %fusion.13 = f32[64,16,512]{2,0,1:T(8,128)S(1)} fusion(f32[64,16,256]{2,0,1:T(8,128)S(1)} %fusion.7, f32[256,256]{1,0:T(8,128)S(1)} %multiply_add_fusion.1, f32[256,256]{1,0:T(8,128)S(1)} %mul.143), kind=kOutput, calls=%fused_computation.29 | convolution fusion | flops 1610743808 | bytes 3670016 | tf_op jit(solution)/shard_map/kzp,pq->kzq/dot_general | solution.py:54
  25.6 5.1 %collective-permute-start.4 = (f32[64,1,256]{2,0,1:T(8,128)S(1)}, f32[64,1,256]{2,0,1:T(8,128)S(1)}, u32[]{:S(2)}, u32[]{:S(2)}) collective-permute-start(f32[64,1,256]{2,0,1:T(8,128)S(1)} %get-tuple-element.4), channel_id=1, source_target_pairs={{0,1},{1,2},{2,3},{3,4},{4,5},{5,6},{6,7},{7,8},{8,9},{9,10},{10,1... | collective-permute-start | bytes 196616 | tf_op jit(solution)/shard_map/ppermute | solution.py:21
  30.7 1.3 collective-permute-start.5
  32.0 1.8 %collective-permute-done.5 = f32[64,1,256]{2,0,1:T(8,128)S(1)} collective-permute-done((f32[64,1,256]{2,0,1:T(8,128)S(1)}, f32[64,1,256]{2,0,1:T(8,128)S(1)}, u32[]{:S(2)}, u32[]{:S(2)}) %collective-permute-start.5) | collective-permute-done | bytes 65568 | tf_op jit(solution)/shard_map/ppermute | solution.py:23
  33.8 0.3 fusion.3
  34.1 1.0 convolution_bitcast_fusion.1
  35.1 45.9 %psum.14 = f32[64,64]{0,1:T(8,128)S(1)} all-reduce(f32[64,64]{0,1:T(8,128)S(1)} %convolution_bitcast_fusion.1), channel_id=1, replica_groups=mesh['sfc'=8,'sub'=4] {'sfc','sub'}, use_global_device_ids=true, to_apply=%region_0.1 | all-reduce | flops 4096 | bytes 32768 | tf_op jit(solution)/shard_map/psum | solution.py:68
  81.1 5.8 %cholesky.44 = f32[64,64]{1,0:T(8,128)S(1)} custom-call(f32[64,64]{1,0:T(8,128)S(1)} %fusion.19), custom_call_target="Cholesky" | custom-call | tf_op jit(solution)/shard_map/jit(cholesky)/cholesky | solution.py:69
  87.0 0.6 compare_reduce_fusion.1
  87.6 0.7 fusion.23
  88.3 4.9 %custom-call.6 = f32[1,64,64]{1,2,0:T(8,128)S(1)} custom-call(f32[1,64,64]{2,1,0:T(8,128)S(1)} %fusion.23), custom_call_target="InvertDiagBlocksLowerTriangular" | custom-call | tf_op jit(solution)/shard_map/triangular_solve/custom-call.0 | solution.py:73
  93.3 1.0 fusion.17
  94.3 1.0 fusion.44
  95.3 40.3 %psum.15 = f32[64,64]{0,1:T(8,128)S(1)} all-reduce(f32[64,64]{0,1:T(8,128)S(1)} %fusion.44), channel_id=1, replica_groups=mesh['sfc'=8,'sub'=4] {'sfc','sub'}, use_global_device_ids=true, to_apply=%region_3.6 | all-reduce | flops 4096 | bytes 32768 | tf_op jit(solution)/shard_map/psum | solution.py:68
  135.7 5.8 %cholesky.55 = f32[64,64]{1,0:T(8,128)S(1)} custom-call(f32[64,64]{1,0:T(8,128)S(1)} %fusion.16), custom_call_target="Cholesky" | custom-call | tf_op jit(solution)/shard_map/jit(cholesky)/cholesky | solution.py:69
  141.6 0.7 compare_reduce_fusion
  142.3 2.2 %convolution_multiply_fusion.1 = f32[64,64]{1,0:T(8,128)} fusion(f32[64,64]{1,0:T(8,128)S(1)} %cholesky.55, f32[64,64]{1,0:T(8,128)S(1)} %cholesky.44, pred[]{:T(512)} %compare_reduce_fusion, pred[]{:T(512)} %compare_reduce_fusion.1), kind=kOutput, calls=%fused_computation.2 | convolution fusion | flops 3174400 | bytes 49154 | tf_op jit(solution)/shard_map/dot_general | solution.py:87
  144.5 0.7 select_bitcast_fusion
  145.2 4.9 %custom-call.7 = f32[1,64,64]{1,2,0:T(8,128)S(1)} custom-call(f32[1,64,64]{2,1,0:T(8,128)S(1)} %select_bitcast_fusion), custom_call_target="InvertDiagBlocksLowerTriangular" | custom-call | tf_op jit(solution)/shard_map/triangular_solve/custom-call.0 | solution.py:73
  150.1 1.1 convolution_multiply_fusion
  151.2 1.3 copy.37
  (25 shorter events, 1.8 us)
Async XLA Ops:
  1.0 1.2 copy-start
  4.5 7.8 %copy-start.1 = (f32[16,256]{1,0:T(8,128)S(1)}, f32[16,256]{1,0:T(8,128)}, u32[]{:S(2)}) copy-start(f32[16,256]{1,0:T(8,128)} %param.6) | copy-start | bytes 49156
  4.7 3.7 %collective-permute-start = (f32[64,1,256]{2,0,1:T(8,128)S(1)}, f32[64,1,256]{2,0,1:T(8,128)S(1)}, u32[]{:S(2)}, u32[]{:S(2)}) collective-permute-start(f32[64,1,256]{2,0,1:T(8,128)S(1)} %get-tuple-element.8), channel_id=1, source_target_pairs={{0,1},{1,2},{2,3},{3,4},{4,5},{5,6},{6,7},{7,8},{8,9},{9,10},{10,1... | collective-permute-start | bytes 196616 | tf_op jit(solution)/shard_map/ppermute | solution.py:21
  7.1 5.2 %collective-permute-start.1 = (f32[64,1,256]{2,0,1:T(8,128)S(1)}, f32[64,1,256]{2,0,1:T(8,128)S(1)}, u32[]{:S(2)}, u32[]{:S(2)}) collective-permute-start(f32[64,1,256]{2,0,1:T(8,128)S(1)} %get-tuple-element.9), channel_id=1, source_target_pairs={{1,0},{2,1},{3,2},{4,3},{5,4},{6,5},{7,6},{8,7},{9,8},{10,9},{11,1... | collective-permute-start | bytes 196616 | tf_op jit(solution)/shard_map/ppermute | solution.py:23
  15.2 6.2 %collective-permute-start.2 = (f32[64,1,256]{2,0,1:T(8,128)S(1)}, f32[64,1,256]{2,0,1:T(8,128)S(1)}, u32[]{:S(2)}, u32[]{:S(2)}) collective-permute-start(f32[64,1,256]{2,0,1:T(8,128)S(1)} %get-tuple-element.6), channel_id=1, source_target_pairs={{0,1},{1,2},{2,3},{3,4},{4,5},{5,6},{6,7},{7,8},{8,9},{9,10},{10,1... | collective-permute-start | bytes 196616 | tf_op jit(solution)/shard_map/ppermute | solution.py:21
  20.0 3.1 %collective-permute-start.3 = (f32[64,1,256]{2,0,1:T(8,128)S(1)}, f32[64,1,256]{2,0,1:T(8,128)S(1)}, u32[]{:S(2)}, u32[]{:S(2)}) collective-permute-start(f32[64,1,256]{2,0,1:T(8,128)S(1)} %get-tuple-element.7), channel_id=1, source_target_pairs={{1,0},{2,1},{3,2},{4,3},{5,4},{6,5},{7,6},{8,7},{9,8},{10,9},{11,1... | collective-permute-start | bytes 196616 | tf_op jit(solution)/shard_map/ppermute | solution.py:23
  25.6 6.4 %collective-permute-start.4 = (f32[64,1,256]{2,0,1:T(8,128)S(1)}, f32[64,1,256]{2,0,1:T(8,128)S(1)}, u32[]{:S(2)}, u32[]{:S(2)}) collective-permute-start(f32[64,1,256]{2,0,1:T(8,128)S(1)} %get-tuple-element.4), channel_id=1, source_target_pairs={{0,1},{1,2},{2,3},{3,4},{4,5},{5,6},{6,7},{7,8},{8,9},{9,10},{10,1... | collective-permute-start | bytes 196616 | tf_op jit(solution)/shard_map/ppermute | solution.py:21
  30.7 3.1 %collective-permute-start.5 = (f32[64,1,256]{2,0,1:T(8,128)S(1)}, f32[64,1,256]{2,0,1:T(8,128)S(1)}, u32[]{:S(2)}, u32[]{:S(2)}) collective-permute-start(f32[64,1,256]{2,0,1:T(8,128)S(1)} %get-tuple-element.5), channel_id=1, source_target_pairs={{1,0},{2,1},{3,2},{4,3},{5,4},{6,5},{7,6},{8,7},{9,8},{10,9},{11,1... | collective-permute-start | bytes 196616 | tf_op jit(solution)/shard_map/ppermute | solution.py:23
where the time goes:
time: 153 us; the launch traced here: 152 us
  blocking collectives  86.2 us (56%)
  other arithmetic  26.6 us (17%)
  starting transfers between devices  16.2 us (11%)
  matrix products  12.2 us (8%)
  waiting for transfers between devices  7.62 us (5%)
  local copies, waits for them, and re-layouts  2.74 us (2%)
    psum x2, blocking collectives, whole_factor(): total = lax.psum(gram, ('sfc', 'sub'))  86.2 us
    another operation x6, other arithmetic, whole_factor(): return jnp.linalg.cholesky(total)  13.1 us
    ppermute x3, starting transfers between devices, with_halo(): lax.ppermute(tail, axis, [(i, (i + 1) % count) for i in range(ends)])  12.4 us
    another operation x4, other arithmetic, lower_solve(): return lax.linalg.triangular_solve(lower, block, left_side=True, lower=True)  11.1 us
    ppermute x3, waiting for transfers between devices, with_halo(): lax.ppermute(head, axis, [((i + 1) % count, i) for i in range(ends)])  7.61 us
    dot_general x3, matrix products, plane_products(): jnp.einsum('kzp,pq->kzq', field, table, precision=lax.Precision.HIGHEST)  5.98 us
    ppermute x3, starting transfers between devices, with_halo(): lax.ppermute(head, axis, [((i + 1) % count, i) for i in range(ends)])  3.88 us
  transfers between devices with their start and end apart: 6, of which 3 were waited for; matrix products, arithmetic and copies ran while one was open for 0% of the time, Pallas kernels for 0%

commit v1 on v0

--- a/solution.py
+++ b/solution.py
@@ -65,7 +65,8 @@
 
 def whole_factor(local):
     gram = jnp.dot(local, local.T, precision=lax.Precision.HIGHEST)
-    total = lax.psum(gram, ("sfc", "sub"))
+    partial = lax.psum(gram, "sub")
+    total = lax.psum(partial, "sfc")
     return jnp.linalg.cholesky(total)
 
 

time: 153 us -> 163 us (1.065)
  blocking collectives: 86.2 us -> 96.3 us
    psum x2 -> x4, blocking collectives: 86.2 us -> 96.3 us  [the longest x2 70.4 us: whole_factor(): total = lax.psum(partial, 'sfc')]
where the time goes in v1:
time: 163 us
  blocking collectives  96.3 us (59%)
  other arithmetic  26.6 us (16%)
  starting transfers between devices  16.2 us (10%)
  matrix products  12.2 us (7%)
  waiting for transfers between devices  7.62 us (5%)
  local copies, waits for them, and re-layouts  2.75 us (2%)
    psum x2, blocking collectives, whole_factor(): total = lax.psum(partial, 'sfc')  70.4 us
    psum x2, blocking collectives, whole_factor(): partial = lax.psum(gram, 'sub')  25.9 us
    another operation x6, other arithmetic, whole_factor(): return jnp.linalg.cholesky(total)  13.1 us
    ppermute x3, starting transfers between devices, with_halo(): lax.ppermute(tail, axis, [(i, (i + 1) % count) for i in range(ends)])  12.4 us
    another operation x4, other arithmetic, lower_solve(): return lax.linalg.triangular_solve(lower, block, left_side=True, lower=True)  11.1 us
    ppermute x3, waiting for transfers between devices, with_halo(): lax.ppermute(head, axis, [((i + 1) % count, i) for i in range(ends)])  7.61 us
    dot_general x3, matrix products, plane_products(): jnp.einsum('kzp,pq->kzq', field, table, precision=lax.Precision.HIGHEST)  5.98 us
    ppermute x3, starting transfers between devices, with_halo(): lax.ppermute(head, axis, [((i + 1) % count, i) for i in range(ends)])  3.88 us
  transfers between devices with their start and end apart: 6, of which 3 were waited for; matrix products, arithmetic and copies ran while one was open for 0% of the time, Pallas kernels for 0%

profile of v1, /device:TPU:0, one launch (start us, length us, event | category | flops | bytes accessed | tf_op | source)
XLA Modules:
  0.0 162.6 jit_solution(15277902875392091801)
XLA Ops:
  1.6 0.5 copy-done
  2.2 2.3 %convolution_bitcast_fusion = f32[64,16,512]{2,0,1:T(8,128)S(1)} fusion(f32[64,16,256]{2,1,0:T(8,128)S(1)} %copy-done, f32[256,256]{1,0:T(8,128)S(1)} %multiply_add_fusion.1, f32[256,256]{1,0:T(8,128)S(1)} %mul.143), kind=kOutput, calls=%fused_computation.1 | convolution fusion | flops 1610743808 | bytes 3670016 | tf_op jit(solution)/shard_map/kzp,pq->kzq/dot_general | solution.py:54
  4.7 2.4 %collective-permute-start = (f32[64,1,256]{2,0,1:T(8,128)S(1)}, f32[64,1,256]{2,0,1:T(8,128)S(1)}, u32[]{:S(2)}, u32[]{:S(2)}) collective-permute-start(f32[64,1,256]{2,0,1:T(8,128)S(1)} %get-tuple-element.8), channel_id=1, source_target_pairs={{0,1},{1,2},{2,3},{3,4},{4,5},{5,6},{6,7},{7,8},{8,9},{9,10},{10,1... | collective-permute-start | bytes 196616 | tf_op jit(solution)/shard_map/ppermute | solution.py:21
  7.1 1.3 collective-permute-start.1
  8.4 3.9 %collective-permute-done.1 = f32[64,1,256]{2,0,1:T(8,128)S(1)} collective-permute-done((f32[64,1,256]{2,0,1:T(8,128)S(1)}, f32[64,1,256]{2,0,1:T(8,128)S(1)}, u32[]{:S(2)}, u32[]{:S(2)}) %collective-permute-start.1) | collective-permute-done | bytes 65568 | tf_op jit(solution)/shard_map/ppermute | solution.py:23
  12.3 0.8 fusion.11
  13.2 1.8 %fusion.14 = f32[64,16,512]{2,0,1:T(8,128)S(1)} fusion(f32[64,16,256]{2,0,1:T(8,128)S(1)} %fusion.11, f32[256,256]{1,0:T(8,128)S(1)} %multiply_add_fusion.1, f32[256,256]{1,0:T(8,128)S(1)} %mul.143), kind=kOutput, calls=%fused_computation.30 | convolution fusion | flops 1610743808 | bytes 3670016 | tf_op jit(solution)/shard_map/kzp,pq->kzq/dot_general | solution.py:54
  15.2 4.8 %collective-permute-start.2 = (f32[64,1,256]{2,0,1:T(8,128)S(1)}, f32[64,1,256]{2,0,1:T(8,128)S(1)}, u32[]{:S(2)}, u32[]{:S(2)}) collective-permute-start(f32[64,1,256]{2,0,1:T(8,128)S(1)} %get-tuple-element.6), channel_id=1, source_target_pairs={{0,1},{1,2},{2,3},{3,4},{4,5},{5,6},{6,7},{7,8},{8,9},{9,10},{10,1... | collective-permute-start | bytes 196616 | tf_op jit(solution)/shard_map/ppermute | solution.py:21
  20.0 1.3 collective-permute-start.3
  21.4 1.8 %collective-permute-done.3 = f32[64,1,256]{2,0,1:T(8,128)S(1)} collective-permute-done((f32[64,1,256]{2,0,1:T(8,128)S(1)}, f32[64,1,256]{2,0,1:T(8,128)S(1)}, u32[]{:S(2)}, u32[]{:S(2)}) %collective-permute-start.3) | collective-permute-done | bytes 65568 | tf_op jit(solution)/shard_map/ppermute | solution.py:23
  23.5 1.8 %fusion.13 = f32[64,16,512]{2,0,1:T(8,128)S(1)} fusion(f32[64,16,256]{2,0,1:T(8,128)S(1)} %fusion.7, f32[256,256]{1,0:T(8,128)S(1)} %multiply_add_fusion.1, f32[256,256]{1,0:T(8,128)S(1)} %mul.143), kind=kOutput, calls=%fused_computation.29 | convolution fusion | flops 1610743808 | bytes 3670016 | tf_op jit(solution)/shard_map/kzp,pq->kzq/dot_general | solution.py:54
  25.6 5.1 %collective-permute-start.4 = (f32[64,1,256]{2,0,1:T(8,128)S(1)}, f32[64,1,256]{2,0,1:T(8,128)S(1)}, u32[]{:S(2)}, u32[]{:S(2)}) collective-permute-start(f32[64,1,256]{2,0,1:T(8,128)S(1)} %get-tuple-element.4), channel_id=1, source_target_pairs={{0,1},{1,2},{2,3},{3,4},{4,5},{5,6},{6,7},{7,8},{8,9},{9,10},{10,1... | collective-permute-start | bytes 196616 | tf_op jit(solution)/shard_map/ppermute | solution.py:21
  30.7 1.3 collective-permute-start.5
  32.0 1.8 %collective-permute-done.5 = f32[64,1,256]{2,0,1:T(8,128)S(1)} collective-permute-done((f32[64,1,256]{2,0,1:T(8,128)S(1)}, f32[64,1,256]{2,0,1:T(8,128)S(1)}, u32[]{:S(2)}, u32[]{:S(2)}) %collective-permute-start.5) | collective-permute-done | bytes 65568 | tf_op jit(solution)/shard_map/ppermute | solution.py:23
  34.1 1.0 convolution_bitcast_fusion.1
  35.1 15.6 %psum.28 = f32[64,64]{0,1:T(8,128)S(1)} all-reduce(f32[64,64]{0,1:T(8,128)S(1)} %convolution_bitcast_fusion.1), channel_id=1, replica_groups=mesh['sfc'=8,'sub'=4] {'sub'}, use_global_device_ids=true, to_apply=%region_0.1 | all-reduce | flops 4096 | bytes 32768 | tf_op jit(solution)/shard_map/psum | solution.py:68
  50.8 37.4 %psum.29 = f32[64,64]{0,1:T(8,128)S(1)} all-reduce(f32[64,64]{0,1:T(8,128)S(1)} %psum.28), channel_id=1, replica_groups=mesh['sfc'=8,'sub'=4] {'sfc'}, use_global_device_ids=true, to_apply=%region_1.2 | all-reduce | flops 4096 | bytes 32768 | tf_op jit(solution)/shard_map/psum | solution.py:69
  88.2 5.8 %cholesky.44 = f32[64,64]{1,0:T(8,128)S(1)} custom-call(f32[64,64]{1,0:T(8,128)S(1)} %fusion.19), custom_call_target="Cholesky" | custom-call | tf_op jit(solution)/shard_map/jit(cholesky)/cholesky | solution.py:70
  94.1 0.6 compare_reduce_fusion.1
  94.7 0.7 fusion.23
  95.4 4.9 %custom-call.6 = f32[1,64,64]{1,2,0:T(8,128)S(1)} custom-call(f32[1,64,64]{2,1,0:T(8,128)S(1)} %fusion.23), custom_call_target="InvertDiagBlocksLowerTriangular" | custom-call | tf_op jit(solution)/shard_map/triangular_solve/custom-call.0 | solution.py:74
  100.4 1.0 fusion.17
  101.5 1.0 fusion.44
  102.4 10.3 %psum.30 = f32[64,64]{0,1:T(8,128)S(1)} all-reduce(f32[64,64]{0,1:T(8,128)S(1)} %fusion.44), channel_id=1, replica_groups=mesh['sfc'=8,'sub'=4] {'sub'}, use_global_device_ids=true, to_apply=%region_4.7 | all-reduce | flops 4096 | bytes 32768 | tf_op jit(solution)/shard_map/psum | solution.py:68
  112.7 33.0 %psum.31 = f32[64,64]{0,1:T(8,128)S(1)} all-reduce(f32[64,64]{0,1:T(8,128)S(1)} %psum.30), channel_id=1, replica_groups=mesh['sfc'=8,'sub'=4] {'sfc'}, use_global_device_ids=true, to_apply=%region_5.8 | all-reduce | flops 4096 | bytes 32768 | tf_op jit(solution)/shard_map/psum | solution.py:69
  145.8 5.8 %cholesky.55 = f32[64,64]{1,0:T(8,128)S(1)} custom-call(f32[64,64]{1,0:T(8,128)S(1)} %fusion.16), custom_call_target="Cholesky" | custom-call | tf_op jit(solution)/shard_map/jit(cholesky)/cholesky | solution.py:70
  151.7 0.7 compare_reduce_fusion
  152.4 2.2 %convolution_multiply_fusion.1 = f32[64,64]{1,0:T(8,128)} fusion(f32[64,64]{1,0:T(8,128)S(1)} %cholesky.55, f32[64,64]{1,0:T(8,128)S(1)} %cholesky.44, pred[]{:T(512)} %compare_reduce_fusion, pred[]{:T(512)} %compare_reduce_fusion.1), kind=kOutput, calls=%fused_computation.2 | convolution fusion | flops 3174400 | bytes 49154 | tf_op jit(solution)/shard_map/dot_general | solution.py:88
  154.6 0.7 select_bitcast_fusion
  155.3 4.9 %custom-call.7 = f32[1,64,64]{1,2,0:T(8,128)S(1)} custom-call(f32[1,64,64]{2,1,0:T(8,128)S(1)} %select_bitcast_fusion), custom_call_target="InvertDiagBlocksLowerTriangular" | custom-call | tf_op jit(solution)/shard_map/triangular_solve/custom-call.0 | solution.py:74
  160.2 1.0 convolution_multiply_fusion
  161.3 1.3 copy.37
  (27 shorter events, 2.5 us)
Async XLA Ops:
  1.0 1.2 copy-start
  4.5 7.8 %copy-start.1 = (f32[16,256]{1,0:T(8,128)S(1)}, f32[16,256]{1,0:T(8,128)}, u32[]{:S(2)}) copy-start(f32[16,256]{1,0:T(8,128)} %param.6) | copy-start | bytes 49156
  4.7 3.7 %collective-permute-start = (f32[64,1,256]{2,0,1:T(8,128)S(1)}, f32[64,1,256]{2,0,1:T(8,128)S(1)}, u32[]{:S(2)}, u32[]{:S(2)}) collective-permute-start(f32[64,1,256]{2,0,1:T(8,128)S(1)} %get-tuple-element.8), channel_id=1, source_target_pairs={{0,1},{1,2},{2,3},{3,4},{4,5},{5,6},{6,7},{7,8},{8,9},{9,10},{10,1... | collective-permute-start | bytes 196616 | tf_op jit(solution)/shard_map/ppermute | solution.py:21
  7.1 5.2 %collective-permute-start.1 = (f32[64,1,256]{2,0,1:T(8,128)S(1)}, f32[64,1,256]{2,0,1:T(8,128)S(1)}, u32[]{:S(2)}, u32[]{:S(2)}) collective-permute-start(f32[64,1,256]{2,0,1:T(8,128)S(1)} %get-tuple-element.9), channel_id=1, source_target_pairs={{1,0},{2,1},{3,2},{4,3},{5,4},{6,5},{7,6},{8,7},{9,8},{10,9},{11,1... | collective-permute-start | bytes 196616 | tf_op jit(solution)/shard_map/ppermute | solution.py:23
  15.2 6.2 %collective-permute-start.2 = (f32[64,1,256]{2,0,1:T(8,128)S(1)}, f32[64,1,256]{2,0,1:T(8,128)S(1)}, u32[]{:S(2)}, u32[]{:S(2)}) collective-permute-start(f32[64,1,256]{2,0,1:T(8,128)S(1)} %get-tuple-element.6), channel_id=1, source_target_pairs={{0,1},{1,2},{2,3},{3,4},{4,5},{5,6},{6,7},{7,8},{8,9},{9,10},{10,1... | collective-permute-start | bytes 196616 | tf_op jit(solution)/shard_map/ppermute | solution.py:21
  20.0 3.1 %collective-permute-start.3 = (f32[64,1,256]{2,0,1:T(8,128)S(1)}, f32[64,1,256]{2,0,1:T(8,128)S(1)}, u32[]{:S(2)}, u32[]{:S(2)}) collective-permute-start(f32[64,1,256]{2,0,1:T(8,128)S(1)} %get-tuple-element.7), channel_id=1, source_target_pairs={{1,0},{2,1},{3,2},{4,3},{5,4},{6,5},{7,6},{8,7},{9,8},{10,9},{11,1... | collective-permute-start | bytes 196616 | tf_op jit(solution)/shard_map/ppermute | solution.py:23
  25.6 6.4 %collective-permute-start.4 = (f32[64,1,256]{2,0,1:T(8,128)S(1)}, f32[64,1,256]{2,0,1:T(8,128)S(1)}, u32[]{:S(2)}, u32[]{:S(2)}) collective-permute-start(f32[64,1,256]{2,0,1:T(8,128)S(1)} %get-tuple-element.4), channel_id=1, source_target_pairs={{0,1},{1,2},{2,3},{3,4},{4,5},{5,6},{6,7},{7,8},{8,9},{9,10},{10,1... | collective-permute-start | bytes 196616 | tf_op jit(solution)/shard_map/ppermute | solution.py:21
  30.7 3.1 %collective-permute-start.5 = (f32[64,1,256]{2,0,1:T(8,128)S(1)}, f32[64,1,256]{2,0,1:T(8,128)S(1)}, u32[]{:S(2)}, u32[]{:S(2)}) collective-permute-start(f32[64,1,256]{2,0,1:T(8,128)S(1)} %get-tuple-element.5), channel_id=1, source_target_pairs={{1,0},{2,1},{3,2},{4,3},{5,4},{6,5},{7,6},{8,7},{9,8},{10,9},{11,1... | collective-permute-start | bytes 196616 | tf_op jit(solution)/shard_map/ppermute | solution.py:23
